TPU v7x, 32 devices: a whole 2x2x4 slice. The times are simulated.
32 devices in a mesh: px: 8 (over y, x, core), py: 4 (over z).
Axes of the slice: x: 2, y: 2, z: 4, core: 2. Of those that a mesh axis runs over, the one named last changes fastest.
Arguments:
- cell_ids: int32 [8, 2560, 128], P('px', 'py'), may hold values from 0 to 262143, as said below
- offset_x: bfloat16 [8, 2560, 128], P('px', 'py'), may hold values from 0 to 1
- offset_y: bfloat16 [8, 2560, 128], P('px', 'py'), may hold values from 0 to 1
- mass: bfloat16 [8, 2560, 128], P('px', 'py'), may hold values from 0.25 to 4
- live: int32 [8, 2560, 128], P('px', 'py'), may hold values from 0 to 1, as said below
- tile_owner: int32 [8, 2560], P('px', 'py'), may hold values from 0 to 7, as said below
- counts: int32 [8, 4, 64], P('px', 'py'), may hold values from 0 to 30720, as said below
Outputs:
- spectrum: float32 [2, 8, 1024, 1024], P(None, None, ('px', 'py'))
- bucket_start: int32 [8, 4, 64], P('px', 'py')
Inputs may be any that keep to these rules, and one draw needn't show every extreme that they name: A device's tiles stand in order of bucket, bucket = tile_owner * 8 + plane. One device has at most 240 tiles of one owner; in every draw, in each column of py, one owner has exactly 240 tiles on every device of that column. `cell_ids`: cell = (plane * 128 + row) * 256 + column, with row inside the owner's block of rows and column inside the device's block of columns; all slots of a tile, padded ones too, carry the tile's plane. In a tile the live particles come first; only the last tile of a bucket on a device has padded slots. counts[i, j, b] is the number of live particles in the tiles of bucket b on device (i, j); in every draw some bucket of every device holds 30720.
All inputs are finite; a program needn't handle non-finite values.
Results may differ from a plain program's by a relative error of at most 0.0003.
The roundings to bfloat16 on the way count: a program that leaves them out, or rounds other values in their place, can miss the bound.
Values may be sent and summed in bfloat16 or wider, within the bound.
A program may use at most 192 MiB of HBM per device.

v0:
```python
import math

import jax
import jax.numpy as jnp
from jax import lax
from jax.sharding import PartitionSpec as P

NX = 1024
NY = 1024
PLANES = 8


BETA = 18.4


def passed_along(value, axis, steps):
    count = lax.axis_size(axis)
    pairs = [(source, (source + steps) % count) for source in range(count)]
    return lax.ppermute(value, axis, pairs)


def entering(value, axis, combine, identity):
    devices, index = (lax.axis_size(axis), lax.axis_index(axis))
    everything = lax.all_gather(value, axis)
    start = jnp.broadcast_to(jnp.asarray(identity, value.dtype), value.shape)

    def step(k, before):
        reached = k < index
        new = combine(before, everything[k])
        return jnp.where(reached, new, before)

    return lax.fori_loop(0, devices, step, start)


def window_weights(local_index, fraction, extent, scaling):
    tap_steps = jnp.arange(-3, 5, dtype=jnp.int32)
    position = (
        tap_steps.astype(jnp.float32)[None, None, :] - fraction.astype(jnp.float32)[:, :, None]
    ) / 4.0
    taps = jnp.exp(BETA * (jnp.sqrt(1.0 - position * position) - 1.0))
    if scaling is not None:
        taps = taps * scaling[:, :, None]
    taps = taps.astype(jnp.bfloat16)
    spot_index = jnp.arange(extent, dtype=jnp.int32)
    offset_step = spot_index[None, None, :] - 4 - local_index[:, :, None]
    placed = jnp.zeros(offset_step.shape, jnp.bfloat16)
    for step_number in range(8):
        placed = jnp.where(
            offset_step == step_number - 3, taps[:, :, step_number : step_number + 1], placed
        )
    return placed


def spread_tiles(tile_cells, frac_x, frac_y, masses, slot_ids, slot_count, row_count, col_count):
    tile_total = tile_cells.shape[0]
    turn_count = max(1, tile_total // 256)
    while tile_total % turn_count != 0:
        turn_count = turn_count - 1
    block_size = tile_total // turn_count

    def add_block(running, pieces):
        block_cells, block_x, block_y, block_mass, block_slot = pieces
        local_y = block_cells % col_count
        local_x = block_cells // col_count % row_count
        weight_x = window_weights(local_x, block_x, row_count + 8, None)
        weight_y = window_weights(local_y, block_y, col_count + 8, block_mass.astype(jnp.float32))
        contrib = jnp.einsum("tna,tnb->tab", weight_x, weight_y, preferred_element_type=jnp.float32)
        return (running.at[block_slot].add(contrib), None)

    stacked = tuple(
        (
            member_array.reshape((turn_count, block_size) + member_array.shape[1:])
            for member_array in (tile_cells, frac_x, frac_y, masses, slot_ids)
        )
    )
    initial = jnp.zeros((slot_count, row_count + 8, col_count + 8), jnp.float32)
    return lax.scan(add_block, initial, stacked)[0]


def fold_rows(extended, row_count):
    core = extended[:, 4 : row_count + 4, :]
    for direction in (1, -1):
        if direction == 1:
            rim_cells = extended[:, row_count + 4 :, :]
        else:
            rim_cells = extended[:, :4, :]
        moved = passed_along(rim_cells, "px", direction)
        if direction == 1:
            core = core.at[:, :4, :].add(moved)
        else:
            core = core.at[:, row_count - 4 :, :].add(moved)
    return core


def fold_columns(extended, col_count):
    core = extended[:, :, 4 : col_count + 4]
    for direction in (1, -1):
        if direction == 1:
            rim_cells = extended[:, :, col_count + 4 :]
        else:
            rim_cells = extended[:, :, :4]
        moved = passed_along(rim_cells, "py", direction)
        if direction == 1:
            core = core.at[:, :, :4].add(moved)
        else:
            core = core.at[:, :, col_count - 4 :].add(moved)
    return core


def add_counts(earlier, later):
    return earlier + later


def project(data_block, table):
    return jnp.einsum("pqy,qk->pyk", data_block, table, precision=lax.Precision.HIGHEST)


def local(cell_ids, offset_x, offset_y, mass, live, tile_owner, counts):
    px_count = lax.axis_size("px")
    py_count = lax.axis_size("py")
    row_count = NX // px_count
    col_count = NY // py_count
    tile_cells = cell_ids[0]
    frac_x = offset_x[0]
    frac_y = offset_y[0]
    masses = jnp.where(live[0] == 1, mass[0], jnp.zeros_like(mass[0]))
    owners = tile_owner[0]
    plane_size = row_count * col_count
    buckets = owners * PLANES + tile_cells[:, 0] // plane_size
    blocks = spread_tiles(
        tile_cells, frac_x, frac_y, masses, buckets, px_count * PLANES, row_count, col_count
    )
    blocks = blocks.reshape((px_count, PLANES) + blocks.shape[1:])
    extended = lax.psum_scatter(blocks, "px", scatter_dimension=0, tiled=True)[0]
    density = fold_columns(fold_rows(extended, row_count), col_count)
    grand_total = lax.psum(jnp.sum(density), ("px", "py"))
    contrast = density / (grand_total / (PLANES * NX * NY)) - 1.0
    by_rows = lax.all_to_all(contrast, "py", split_axis=1, concat_axis=2, tiled=True)
    part_rows = by_rows.shape[1]
    freq_y = jnp.arange(NY, dtype=jnp.int32)
    angle_y = 2.0 * math.pi / NY * (freq_y[:, None] * freq_y[None, :] % NY).astype(jnp.float32)
    flat_rows = by_rows.reshape(-1, NY)
    real_y = jnp.dot(flat_rows, jnp.cos(angle_y), precision=lax.Precision.HIGHEST).reshape(
        by_rows.shape
    )
    imag_y = -jnp.dot(flat_rows, jnp.sin(angle_y), precision=lax.Precision.HIGHEST).reshape(
        by_rows.shape
    )
    real_cols, imag_cols = (
        lax.all_to_all(
            lax.all_to_all(real_y, "px", split_axis=2, concat_axis=1, tiled=True),
            "py",
            split_axis=2,
            concat_axis=1,
            tiled=True,
        ),
        lax.all_to_all(
            lax.all_to_all(imag_y, "px", split_axis=2, concat_axis=1, tiled=True),
            "py",
            split_axis=2,
            concat_axis=1,
            tiled=True,
        ),
    )
    row_order = jnp.arange(NX, dtype=jnp.int32)
    within = row_order % part_rows
    from_px = row_order // part_rows % px_count
    from_py = row_order // (part_rows * px_count)
    true_x = from_px * row_count + from_py * part_rows + within
    angle_x = 2.0 * math.pi / NX * (true_x[:, None] * row_order[None, :] % NX).astype(jnp.float32)
    cos_x = jnp.cos(angle_x)
    sin_x = jnp.sin(angle_x)
    out_real = project(real_cols, cos_x) + project(imag_cols, sin_x)
    out_imag = project(imag_cols, cos_x) - project(real_cols, sin_x)
    spectrum = jnp.stack([out_real, out_imag]) * (1.0 / math.sqrt(NX * NY))
    earlier_sum = entering(counts, "px", add_counts, jnp.zeros_like(counts))
    column_sum = lax.psum(counts, "px")
    preceding = jnp.cumsum(column_sum, axis=-1) - column_sum
    bucket_start = (preceding + earlier_sum).astype(jnp.int32)
    return (spectrum, bucket_start)


def solution(mesh):
    placed = (
        P("px", "py", None),
        P("px", "py", None),
        P("px", "py", None),
        P("px", "py", None),
        P("px", "py", None),
        P("px", "py"),
        P("px", "py", None),
    )
    return jax.shard_map(
        local,
        mesh=mesh,
        in_specs=placed,
        out_specs=(P(None, None, ("px", "py"), None), P("px", "py", None)),
        check_vma=False,
    )
```

profile of v0, /device:TPU:0, one launch (start us, length us, event | category | flops | bytes accessed | tf_op | source)
XLA Modules:
  0.0 875.2 jit_solution(6027236475917592853)
XLA Ops:
  10.4 5.6 broadcast_in_dim.269
  16.0 417.2 %while.31 = (s32[]{:T(128)}, f32[64,136,264]{2,1,0:T(8,128)}, s32[2,320]{1,0:T(2,128)S(1)}, s32[2,320,128]{2,1,0:T(8,128)S(1)}, bf16[2,320,128]{2,1,0:T(8,128)(2...) while((s32[]{:T(128)}, f32[64,136,264]{2,1,0:T(8,128)}, ...), condition=%wide.region_2.3_spmd, body=%wide.region_0.2_spmd.sunk | while | flops 3237786880 | bytes 193993872 | solution.py:77
  19.7 44.1 %fusion.176 = f32[320,136,264]{2,1,0:T(8,128)} fusion(s32[320,128]{1,0:T(8,128)S(1)} %add_select_fusion.11, s32[264]{0:T(512)S(1)} %iota_add_fusion.4, s32[320,128]{1,0:T(8,128)S(1)} %get-tuple-element.422, s32[136]{0:T(256)S(1)} %iota_add_fusion.5, bf16[320,128]{1,0:T(8,128)(2,1)S(1)} %get-tuple-element.426, ...), kind=kOutput, calls=%fused_computation.35.clone.1 | convolution fusion | flops 3219783680 | bytes 47597120 | tf_op jit(solution)/shard_map/while/body/eval_jaxpr/tna,tnb->tab/dot_general | solution.py:67
  63.8 167.5 %scatter_fusion = f32[64,136,264]{2,1,0:T(8,128)} fusion(f32[64,136,264]{2,1,0:T(8,128)} %get-tuple-element.456, s32[320]{0:T(512)S(1)} %fusion.175, f32[320,136,264]{2,1,0:T(8,128)} %fusion.176), kind=kCustom, calls=%fused_computation.clone.1 | custom fusion | flops 11489280 | bytes 137872640 | tf_op jit(solution)/shard_map/while/body/eval_jaxpr/scatter-add | solution.py:68
  235.1 44.1 %fusion.176 = f32[320,136,264]{2,1,0:T(8,128)} fusion(s32[320,128]{1,0:T(8,128)S(1)} %add_select_fusion.11, s32[264]{0:T(512)S(1)} %iota_add_fusion.4, s32[320,128]{1,0:T(8,128)S(1)} %get-tuple-element.422, s32[136]{0:T(256)S(1)} %iota_add_fusion.5, bf16[320,128]{1,0:T(8,128)(2,1)S(1)} %get-tuple-element.426, ...), kind=kOutput, calls=%fused_computation.35.clone.1 | convolution fusion | flops 3219783680 | bytes 47597120 | tf_op jit(solution)/shard_map/while/body/eval_jaxpr/tna,tnb->tab/dot_general | solution.py:67
  279.2 154.0 %scatter_fusion = f32[64,136,264]{2,1,0:T(8,128)} fusion(f32[64,136,264]{2,1,0:T(8,128)} %get-tuple-element.456, s32[320]{0:T(512)S(1)} %fusion.175, f32[320,136,264]{2,1,0:T(8,128)} %fusion.176), kind=kCustom, calls=%fused_computation.clone.1 | custom fusion | flops 11489280 | bytes 137872640 | tf_op jit(solution)/shard_map/while/body/eval_jaxpr/scatter-add | solution.py:68
  433.2 96.0 %reduce-scatter.2.cloned.1.call-done = f32[1,8,136,264]{3,2,1,0:T(8,128)} async-done(((f32[8,8,136,264]{3,2,1,0:T(8,128)}), f32[1,8,136,264]{3,2,1,0:T(8,128)}) %reduce-scatter.2.cloned.1.call-update) | async-done | bytes 1148944 | tf_op jit(solution)/shard_map/reduce_scatter | solution.py:134
  541.0 12.2 %collective-permute-done.2 = f32[8,128,4]{2,1,0:T(8,128)S(1)} collective-permute-done((f32[8,128,4]{2,1,0:T(8,128)S(1)}, f32[8,128,4]{2,1,0:T(8,128)S(1)}, u32[]{:S(2)}, u32[]{:S(2)}) %collective-permute-start.2) | collective-permute-done | bytes 16416 | tf_op jit(solution)/shard_map/ppermute | solution.py:19
  554.9 9.2 %collective-permute-done.3 = f32[8,128,4]{2,1,0:T(8,128)S(1)} collective-permute-done((f32[8,128,4]{2,1,0:T(8,128)S(1)}, f32[8,128,4]{2,1,0:T(8,128)S(1)}, u32[]{:S(2)}, u32[]{:S(2)}) %collective-permute-start.3) | collective-permute-done | bytes 16416 | tf_op jit(solution)/shard_map/ppermute | solution.py:19
  567.7 38.4 %psum.14 = f32[]{:T(128)} all-reduce(f32[]{:T(128)} %reduce_sum.9), channel_id=1, replica_groups=mesh['px'=8,'py'=4] {'px','py'}, use_global_device_ids=true, to_apply=%region_5.6 | all-reduce | flops 1 | bytes 8 | tf_op jit(solution)/shard_map/psum | solution.py:136
  607.5 27.8 %all_to_all.87 = f32[8,128,256]{2,0,1:T(8,128)S(1)} all-to-all(f32[8,128,256]{2,0,1:T(8,128)S(1)} %copy.29), channel_id=1, replica_groups=mesh['px'=8,'py'=4] {'py'}, dimensions={1} | all-to-all | bytes 2097152 | tf_op jit(solution)/shard_map/all_to_all | solution.py:138
  636.6 20.0 %fusion.105 = f32[8,32,1024]{2,1,0:T(8,128)S(1)} fusion(f32[8,32,1024]{2,1,0:T(8,128)S(1)} %dot_general.27), kind=kOutput, calls=%fused_computation.158 | convolution fusion | flops 3236167680 | bytes 2097152 | tf_op jit(solution)/shard_map/dot_general | solution.py:146
  659.3 4.8 reshape.352
  664.1 15.4 %all-to-all-start.3 = ((f32[8,1,32768]{2,1,0:T(1,128)}), f32[8,1,32768]{2,1,0:T(1,128)S(1)}, u32[]{:S(2)}, u32[]{:S(2)}) async-start(f32[8,1,32768]{2,1,0:T(1,128)} %reshape.352), calls=%async_computation.4 | async-start | bytes 2097152 | tf_op jit(solution)/shard_map/all_to_all | solution.py:158
  679.5 20.0 %fusion.87 = f32[8,32,1024]{2,1,0:T(8,128)S(1)} fusion(f32[8,32,1024]{2,1,0:T(8,128)S(1)} %dot_general.27), kind=kOutput, calls=%fused_computation.145 | convolution fusion | flops 3235905536 | bytes 2097152 | tf_op jit(solution)/shard_map/dot_general | solution.py:143
  702.2 4.8 reshape.350
  730.0 6.4 psum.15
  736.7 8.7 all-gather
  756.0 5.0 all-to-all-start.2
  763.5 23.8 %all-to-all-done.2 = f32[8,256,128]{1,0,2:T(8,128)S(1)} async-done(((f32[8,256,128]{1,0,2:T(8,128)}), f32[8,256,128]{1,0,2:T(8,128)S(1)}, u32[]{:S(2)}, u32[]{:S(2)}) %all-to-all-start.2) | async-done | bytes 1048608 | tf_op jit(solution)/shard_map/all_to_all | solution.py:150
  788.5 19.4 %fusion.79 = f32[8,32,1024]{2,1,0:T(8,128)S(1)} fusion(f32[8,1024,32]{1,2,0:T(8,128)S(1)} %all_to_all.81, s32[1024]{0:T(1024)S(1)} %fusion.131), kind=kOutput, calls=%fused_computation.137 | convolution fusion | flops 3235905536 | bytes 2101248 | tf_op jit(solution)/shard_map/pqy,qk->pyk/dot_general | solution.py:115
  807.9 19.8 %fusion.77 = f32[8,32,1024]{2,1,0:T(8,128)S(1)} fusion(f32[8,1024,32]{1,2,0:T(8,128)S(1)} %all_to_all.73, s32[1024]{0:T(1024)S(1)} %fusion.131), kind=kOutput, calls=%fused_computation.135 | convolution fusion | flops 3235905536 | bytes 2101248 | tf_op jit(solution)/shard_map/pqy,qk->pyk/dot_general | solution.py:115
  827.7 19.4 %fusion.111 = f32[1,8,32,1024]{3,2,1,0:T(8,128)S(1)} fusion(f32[8,32,1024]{2,1,0:T(8,128)S(1)} %fusion.79, f32[8,1024,32]{1,2,0:T(8,128)S(1)} %all_to_all.73, s32[1024]{0:T(1024)S(1)} %fusion.131), kind=kOutput, calls=%fused_computation.160 | convolution fusion | flops 3236167680 | bytes 3149824 | tf_op jit(solution)/shard_map/pqy,qk->pyk/dot_general | solution.py:115
  847.1 19.3 %fusion.117 = f32[1,8,32,1024]{3,2,1,0:T(8,128)S(1)} fusion(f32[8,32,1024]{2,1,0:T(8,128)S(1)} %fusion.77, f32[8,1024,32]{1,2,0:T(8,128)S(1)} %all_to_all.81, s32[1024]{0:T(1024)S(1)} %fusion.131), kind=kOutput, calls=%fused_computation.162 | convolution fusion | flops 3236167680 | bytes 3149824 | tf_op jit(solution)/shard_map/pqy,qk->pyk/dot_general | solution.py:115
  (101 shorter events, 74.1 us)
Async XLA Ops:
  7.2 522.0 %reduce-scatter.2.cloned.1.call-start = ((), (), s32[]{:S(2)}) async-start(), calls=%async_computation.6 | async-start | bytes 15040512 | tf_op jit(solution)/shard_map/reduce_scatter | solution.py:134
  10.3 5.6 copy-start
  16.0 47.8 %copy-start.2 = (bf16[2,320,128]{2,1,0:T(8,128)(2,1)}, bf16[2,320,128]{2,1,0:T(8,128)(2,1)S(1)}, u32[]{:S(2)}) copy-start(bf16[2,320,128]{2,1,0:T(8,128)(2,1)S(1)} %get-tuple-element.469) | copy-start | bytes 491524 | tf_op jit(solution)/shard_map/while
  63.8 167.5 %copy-start.1 = (s32[1,640,128]{2,1,0:T(8,128)S(1)}, s32[1,640,128]{2,1,0:T(8,128)}, u32[]{:S(2)}) copy-start(s32[1,640,128]{2,1,0:T(8,128)} %get-tuple-element.500) | copy-start | bytes 983044 | tf_op jit(solution)/shard_map/while
  63.8 167.5 %copy-start.3 = (bf16[2,320,128]{2,1,0:T(8,128)(2,1)S(1)}, bf16[2,320,128]{2,1,0:T(8,128)(2,1)}, u32[]{:S(2)}) copy-start(bf16[2,320,128]{2,1,0:T(8,128)(2,1)} %copy-done.2) | copy-start | bytes 491524 | tf_op jit(solution)/shard_map/while
  231.3 47.8 %copy-start.2 = (bf16[2,320,128]{2,1,0:T(8,128)(2,1)}, bf16[2,320,128]{2,1,0:T(8,128)(2,1)S(1)}, u32[]{:S(2)}) copy-start(bf16[2,320,128]{2,1,0:T(8,128)(2,1)S(1)} %get-tuple-element.469) | copy-start | bytes 491524 | tf_op jit(solution)/shard_map/while
  279.2 154.0 %copy-start.1 = (s32[1,640,128]{2,1,0:T(8,128)S(1)}, s32[1,640,128]{2,1,0:T(8,128)}, u32[]{:S(2)}) copy-start(s32[1,640,128]{2,1,0:T(8,128)} %get-tuple-element.500) | copy-start | bytes 983044 | tf_op jit(solution)/shard_map/while
  279.2 154.0 %copy-start.3 = (bf16[2,320,128]{2,1,0:T(8,128)(2,1)S(1)}, bf16[2,320,128]{2,1,0:T(8,128)(2,1)}, u32[]{:S(2)}) copy-start(bf16[2,320,128]{2,1,0:T(8,128)(2,1)} %copy-done.2) | copy-start | bytes 491524 | tf_op jit(solution)/shard_map/while
  530.1 4.5 collective-permute-start
  531.8 4.4 collective-permute-start.1
  536.4 16.7 %collective-permute-start.2 = (f32[8,128,4]{2,1,0:T(8,128)S(1)}, f32[8,128,4]{2,1,0:T(8,128)S(1)}, u32[]{:S(2)}, u32[]{:S(2)}) collective-permute-start(f32[8,128,4]{2,1,0:T(8,128)S(1)} %get-tuple-element.334), channel_id=1, source_target_pairs={{0,1},{1,2},{2,3},{3,0},{4,5},{5,6},{6,7},{7,4},{8,9},{9,10},{10,1... | collective-permute-start | bytes 49160 | tf_op jit(solution)/shard_map/ppermute | solution.py:19
  538.3 25.8 %collective-permute-start.3 = (f32[8,128,4]{2,1,0:T(8,128)S(1)}, f32[8,128,4]{2,1,0:T(8,128)S(1)}, u32[]{:S(2)}, u32[]{:S(2)}) collective-permute-start(f32[8,128,4]{2,1,0:T(8,128)S(1)} %get-tuple-element.333), channel_id=1, source_target_pairs={{0,3},{1,0},{2,1},{3,2},{4,7},{5,4},{6,5},{7,6},{8,11},{9,8},{10,9... | collective-permute-start | bytes 49160 | tf_op jit(solution)/shard_map/ppermute | solution.py:19
  664.1 43.0 %all-to-all-start.3 = ((f32[8,1,32768]{2,1,0:T(1,128)}), f32[8,1,32768]{2,1,0:T(1,128)S(1)}, u32[]{:S(2)}, u32[]{:S(2)}) async-start(f32[8,1,32768]{2,1,0:T(1,128)} %reshape.352), calls=%async_computation.4 | async-start | bytes 2097152 | tf_op jit(solution)/shard_map/all_to_all | solution.py:158
  707.0 19.4 %all-to-all-start.1 = ((f32[8,1,32768]{2,1,0:T(1,128)}), f32[8,1,32768]{2,1,0:T(1,128)S(1)}, u32[]{:S(2)}, u32[]{:S(2)}) async-start(f32[8,1,32768]{2,1,0:T(1,128)} %reshape.350), calls=%async_computation.2 | async-start | bytes 2097152 | tf_op jit(solution)/shard_map/all_to_all | solution.py:151
  718.0 12.0 %copy-start.4 = (s32[1,1,64]{2,1,0:T(1,128)S(1)}, s32[1,1,64]{2,1,0:T(1,128)}, u32[]{:S(2)}) copy-start(s32[1,1,64]{2,1,0:T(1,128)} %param.25) | copy-start | bytes 772
  726.4 29.6 %all-to-all-start.4 = ((f32[8,256,128]{1,0,2:T(8,128)}), f32[8,256,128]{1,0,2:T(8,128)S(1)}, u32[]{:S(2)}, u32[]{:S(2)}) async-start(f32[8,256,128]{1,0,2:T(8,128)} %copy.41), calls=%async_computation.5 | async-start | bytes 2097152 | tf_op jit(solution)/shard_map/all_to_all | solution.py:157
  756.0 31.3 %all-to-all-start.2 = ((f32[8,256,128]{1,0,2:T(8,128)}), f32[8,256,128]{1,0,2:T(8,128)S(1)}, u32[]{:S(2)}, u32[]{:S(2)}) async-start(f32[8,256,128]{1,0,2:T(8,128)} %copy.35), calls=%async_computation.3 | async-start | bytes 2097152 | tf_op jit(solution)/shard_map/all_to_all | solution.py:150
Sparse Core Ops, SparseCore 0:
  433.3 95.7 reduce-scatter.1
where the time goes:
time: 882 us; the launch traced here: 875 us
  other arithmetic  342 us (39%)
  matrix products  206 us (23%)
  waiting for transfers between devices  146 us (17%)
  blocking collectives  81.4 us (9%)
  local copies, waits for them, and re-layouts  49.1 us (6%)
  starting transfers between devices  34.9 us (4%)
  between operations  15.4 us (2%)
    scatter-add x2, other arithmetic, add_block(): return (running.at[block_slot].add(contrib), None)  321 us
    reduce_scatter x1, waiting for transfers between devices, local(): lax.psum_scatter(blocks, 'px', scatter_dimension=0, tiled=True)[0]  96 us
    dot_general x2, matrix products, add_block(): jnp.einsum('tna,tnb->tab', weight_x, weight_y, preferred_element_type=jnp...  88.1 us
    dot_general x4, matrix products, project(): jnp.einsum('pqy,qk->pyk', data_block, table, precision=lax.Precision.HIGH...  77.9 us
    psum x1, blocking collectives, local(): grand_total = lax.psum(jnp.sum(density), ('px', 'py'))  38.4 us
    all_to_all x1, blocking collectives, local(): lax.all_to_all(contrast, 'py', split_axis=1, concat_axis=2, tiled=True)  27.8 us
    all_to_all x1, waiting for transfers between devices, local(): lax.all_to_all(lax.all_to_all(real_y, 'px', split_axis=2, concat_axis=1,...  23.8 us
    ppermute x4, waiting for transfers between devices, passed_along(): return lax.ppermute(value, axis, pairs)  22.2 us
  transfers between devices with their start and end apart: 9, of which 7 were waited for; matrix products, arithmetic and copies ran while one was open for 6% of the time, Pallas kernels for 0%

commit v1 on v0

v1 whole, which is shorter than its diff:
```python
import functools
import math

import jax
import jax.numpy as jnp
import numpy as np
from jax import lax
from jax.experimental import pallas as pl
from jax.experimental.pallas import tpu as pltpu
from jax.sharding import PartitionSpec as P

NX = 1024
NY = 1024
PLANES = 8
BETA = 18.4
LANES = 128
GROUP = 4


def tap_blocks(start, fraction, scaling):
    rows = lax.broadcasted_iota(jnp.int32, (8, LANES), 0)
    first = jnp.broadcast_to(start, (8, LANES)) - 3
    depth = (rows - first) & 7
    z = ((depth - 3).astype(jnp.float32) - fraction) * 0.25
    taps = jnp.exp(BETA * (jnp.sqrt(jnp.maximum(1.0 - z * z, 0.0)) - 1.0))
    if scaling is not None:
        taps = taps * scaling
    block = (first + depth) >> 3
    odd = (block & 1) == 1
    zero = jnp.zeros_like(taps)
    both = jnp.concatenate(
        [jnp.where(odd, zero, taps), jnp.where(odd, taps, zero)], axis=0
    ).astype(jnp.bfloat16)
    half = block >> 1
    return both, half


def spread_kernel(row_count, col_count, bucket_count, starts_ref, lx_ref, ly_ref, fx_ref, fy_ref,
                  w_ref, out_ref, acc_ref, wx_ref, wy_ref):
    col_blocks = col_count // 16
    lane_tiles = NX // LANES
    out_ref[...] = jnp.zeros_like(out_ref)
    wx_ref[...] = jnp.zeros_like(wx_ref)
    height = col_count + 16
    lane = lax.broadcasted_iota(jnp.int32, (height, LANES), 1)

    def bucket(b, _):
        begin = starts_ref[b]
        end = starts_ref[b + 1]
        chunks = (end - begin + GROUP - 1) // GROUP

        @pl.when(chunks > 0)
        def _():
            acc_ref[...] = jnp.zeros_like(acc_ref)

            def chunk(c, _):
                for g in range(GROUP):
                    t = begin + c * GROUP + g
                    at = pl.ds(t, 1)
                    scale = jnp.where(t < end, 1.0, 0.0)
                    taps, block = tap_blocks(lx_ref[at, :], fx_ref[at, :], None)
                    block = jnp.concatenate([block, block], axis=0).astype(jnp.int16)
                    none = jnp.zeros_like(taps)
                    cols = pl.ds(g * LANES, LANES)
                    for k in range(9):
                        wx_ref[pl.ds(k * 16, 16), cols] = jnp.where(block == k, taps, none)
                    wx_ref[pl.ds(240, 16), cols] = jnp.where(block == -1, taps, none)
                    taps, block = tap_blocks(ly_ref[at, :], fy_ref[at, :], w_ref[at, :] * scale)
                    block = jnp.where(block < 0, col_blocks, block)
                    block = jnp.concatenate([block, block], axis=0).astype(jnp.int16)
                    for k in range(col_blocks + 1):
                        wy_ref[pl.ds(k * 16, 16), cols] = jnp.where(block == k, taps, none)
                acc_ref[...] += lax.dot_general(
                    wy_ref[...], wx_ref[...], (((1,), (1,)), ((), ())),
                    preferred_element_type=jnp.float32,
                )
                return 0

            lax.fori_loop(0, chunks, chunk, 0)
            plane = b % PLANES
            tile = (b // PLANES * row_count) // LANES
            here = pl.ds(pl.multiple_of(tile * LANES, LANES), LANES)
            after = pl.ds(pl.multiple_of((tile + 1) % lane_tiles * LANES, LANES), LANES)
            before = pl.ds(pl.multiple_of((tile + lane_tiles - 1) % lane_tiles * LANES, LANES), LANES)
            out_ref[plane, :, here] += acc_ref[:, :LANES]
            rim = acc_ref[:, LANES:]
            out_ref[plane, :, after] += jnp.where(lane < 64, rim, 0.0)
            out_ref[plane, :, before] += jnp.where(lane < 64, 0.0, rim)
        return 0

    lax.fori_loop(0, bucket_count, bucket, 0)


def spread(starts, lx, ly, fx, fy, w, row_count, col_count):
    height = col_count + 16
    bucket_count = starts.shape[0] - 1
    vmem = pl.BlockSpec(memory_space=pltpu.VMEM)
    return pl.pallas_call(
        functools.partial(spread_kernel, row_count, col_count, bucket_count),
        out_shape=jax.ShapeDtypeStruct((PLANES, height, NX), jnp.float32),
        in_specs=[pl.BlockSpec(memory_space=pltpu.SMEM)] + [vmem] * 5,
        out_specs=vmem,
        scratch_shapes=[
            pltpu.VMEM((height, 2 * LANES), jnp.float32),
            pltpu.VMEM((2 * LANES, GROUP * LANES), jnp.bfloat16),
            pltpu.VMEM((height, GROUP * LANES), jnp.bfloat16),
        ],
        compiler_params=pltpu.CompilerParams(vmem_limit_bytes=40 * 1024 * 1024),
        name="spread",
    )(starts, lx, ly, fx, fy, w)


def split(value):
    high = lax.reduce_precision(value, 8, 7)
    return high.astype(jnp.bfloat16), (value - high).astype(jnp.bfloat16)


def dft_tables():
    n = np.arange(NX)
    k = np.arange(32)
    coarse = 2.0 * np.pi / NX * ((32 * k[:, None] * n[None, :]) % NX)
    fine = 2.0 * np.pi / NX * ((k[:, None] * n[None, :]) % NX)
    cc, cs, fc, fs = lax.optimization_barrier(
        tuple(jnp.asarray(f(a), jnp.float32) for a in (coarse, fine) for f in (np.cos, np.sin))
    )
    cc, cs = cc[:, None, :], cs[:, None, :]
    fc, fs = fc[None, :, :], fs[None, :, :]
    cosine = (cc * fc - cs * fs).reshape(NX, NX)
    sine = (cs * fc + cc * fs).reshape(NX, NX)
    return split(cosine) + split(sine)


def dot(a, b):
    return jnp.dot(a, b, preferred_element_type=jnp.float32)


def local(cell_ids, offset_x, offset_y, mass, live, tile_owner, counts):
    px_count = lax.axis_size("px")
    py_count = lax.axis_size("py")
    row_count = NX // px_count
    col_count = NY // py_count
    parts = px_count // PLANES
    cells = cell_ids[0]
    owners = tile_owner[0]
    buckets = owners * PLANES + cells[:, 0] // (row_count * col_count)
    edges = jnp.arange(px_count * PLANES + 1, dtype=jnp.int32)
    starts = jnp.sum((buckets[None, :] < edges[:, None]).astype(jnp.int32), axis=1)

    def padded(value):
        return jnp.pad(value, ((0, 8), (0, 0)))

    ly = padded(cells % col_count)
    lx = padded((cells // col_count % row_count + owners[:, None] * row_count) % LANES)
    fx = padded(offset_x[0].astype(jnp.float32))
    fy = padded(offset_y[0].astype(jnp.float32))
    w = padded(jnp.where(live[0] == 1, mass[0], jnp.zeros_like(mass[0])).astype(jnp.float32))
    grid = spread(starts, lx, ly, fx, fy, w, row_count, col_count)
    height = col_count + 16
    width = NX // parts
    if parts > 1:
        grid = grid.reshape(PLANES, height, parts, width).transpose(0, 2, 1, 3)
        grid = grid.reshape(px_count, height, width)
    mine = lax.psum_scatter(grid, "px", scatter_dimension=0, tiled=True)[0]
    total = lax.psum(jnp.sum(mine), ("px", "py"))
    by_cols = lax.all_to_all(mine, "py", split_axis=1, concat_axis=0, tiled=True)
    part = width // py_count
    ext = by_cols.reshape(py_count, height, part)
    core = ext[:, :col_count]
    right = jnp.roll(ext[:, col_count : col_count + 4], 1, axis=0)
    left = jnp.roll(ext[:, col_count + 12 :], -1, axis=0)
    core = core + jnp.concatenate(
        [right, jnp.zeros((py_count, col_count - 8, part), jnp.float32), left], axis=1
    )
    data = core.reshape(NY, part)
    cos_hi, cos_lo, sin_hi, sin_lo = dft_tables()
    hi, lo = split(data)
    both = jnp.concatenate([hi, lo], axis=1)
    real = dot(cos_hi, both)
    real = real[:, :part] + real[:, part:] + dot(cos_lo, hi)
    imag = dot(sin_hi, both)
    imag = -(imag[:, :part] + imag[:, part:] + dot(sin_lo, hi))
    devices = px_count * py_count
    ky_part = NY // devices
    lines = jnp.stack([real, imag]).reshape(2, devices, ky_part, part).transpose(1, 0, 2, 3)
    got = lax.all_to_all(lines, ("px", "py"), split_axis=0, concat_axis=0, tiled=True)
    got = got.reshape(PLANES, parts * py_count, 2, ky_part, part).transpose(2, 0, 3, 1, 4)
    got = got.reshape(2 * PLANES * ky_part, NX)
    hi, lo = split(got)
    rows = PLANES * ky_part
    both = jnp.concatenate([hi, lo], axis=0)
    by_cos = dot(both, cos_hi)
    by_cos = by_cos[: 2 * rows] + by_cos[2 * rows :] + dot(hi, cos_lo)
    by_sin = dot(both, sin_hi)
    by_sin = by_sin[: 2 * rows] + by_sin[2 * rows :] + dot(hi, sin_lo)
    out = jnp.stack([by_cos[:rows] + by_sin[rows:], by_cos[rows:] - by_sin[:rows]])
    out = out.reshape(2, PLANES, ky_part, NX)
    norm = 1.0 / math.sqrt(NX * NY)
    index = lax.axis_index("px") * py_count + lax.axis_index("py")
    shape = (2, 1, ky_part, NX)
    at_zero = (
        (lax.broadcasted_iota(jnp.int32, shape, 0) == 0)
        & (lax.broadcasted_iota(jnp.int32, shape, 2) + index == 0)
        & (lax.broadcasted_iota(jnp.int32, shape, 3) == 0)
    )
    spectrum = out * (PLANES * NX * NY * norm / total) - jnp.where(at_zero, NX * NY * norm, 0.0)
    column = lax.all_gather(counts, "px")
    column_sum = jnp.sum(column, axis=0)
    reached = lax.broadcasted_iota(jnp.int32, column.shape, 0) < lax.axis_index("px")
    earlier = jnp.sum(jnp.where(reached, column, 0), axis=0)
    preceding = jnp.cumsum(column_sum, axis=-1) - column_sum
    bucket_start = (preceding + earlier).astype(jnp.int32)
    return (spectrum, bucket_start)


def solution(mesh):
    placed = (
        P("px", "py", None),
        P("px", "py", None),
        P("px", "py", None),
        P("px", "py", None),
        P("px", "py", None),
        P("px", "py"),
        P("px", "py", None),
    )
    return jax.shard_map(
        local,
        mesh=mesh,
        in_specs=placed,
        out_specs=(P(None, None, ("px", "py"), None), P("px", "py", None)),
        check_vma=False,
    )
```

time: 882 us -> 298 us (0.34)
  other arithmetic: 342 us -> 14.3 us
  matrix products: 206 us -> 11.1 us
  Pallas kernels: 0 us -> 67.5 us
  waiting for transfers between devices: 146 us -> 100 us
  local copies, waits for them, and re-layouts: 49.1 us -> 14.6 us
  starting transfers between devices: 34.9 us -> 7.48 us
  blocking collectives: 81.4 us -> 67 us
    scatter-add x4 -> x0, other arithmetic: 322 us -> none  [the longest x2 321 us: add_block(): return (running.at[block_slot].add(contrib), None)]
    dot_general x8, matrix products: 206 us -> 11.1 us  [dot(): return jnp.dot(a, b, preferred_element_type=jnp.float32)]
    pallas_call x0 -> x1, Pallas kernels: none -> 67.5 us  [spread(): pl.pallas_call(functools.partial(spread_kernel, row_count, col_count, buc...]
    all_to_all x1 -> x0, blocking collectives: 27.8 us -> none  [local(): lax.all_to_all(contrast, 'py', split_axis=1, concat_axis=2, tiled=True)]
    ppermute x4 -> x0, waiting for transfers between devices: 22.2 us -> none  [passed_along(): return lax.ppermute(value, axis, pairs)]
    all_to_all x4 -> x2, starting transfers between devices: 28 us -> 7.44 us  [the longest x1 4.58 us: local(): lax.all_to_all(mine, 'py', split_axis=1, concat_axis=0, tiled=True)]
    reduce_scatter x1, waiting for transfers between devices: 96 us -> 78 us  [local(): mine = lax.psum_scatter(grid, 'px', scatter_dimension=0, tiled=True)[0]]
    all_to_all x10 -> x2, local copies, waits for them, and re-layouts: 12 us -> 3 us  [local(): lax.all_to_all(mine, 'py', split_axis=1, concat_axis=0, tiled=True)]
  transfers between devices with their start and end apart: 9 -> 3, of which waited for: 7 -> 2; matrix products, arithmetic and copies ran while one was open for 6% -> 2% of each run, Pallas kernels for 0% -> 0%
where the time goes in v1:
time: 298 us; the launch traced here: 297 us
  waiting for transfers between devices  100 us (34%)
  Pallas kernels  67.5 us (23%)
  blocking collectives  67 us (22%)
  between operations  15 us (5%)
  local copies, waits for them, and re-layouts  14.6 us (5%)
  other arithmetic  14.3 us (5%)
  matrix products  11.1 us (4%)
  starting transfers between devices  7.48 us (3%)
    reduce_scatter x1, waiting for transfers between devices, local(): mine = lax.psum_scatter(grid, 'px', scatter_dimension=0, tiled=True)[0]  78 us
    pallas_call x1, Pallas kernels, spread(): pl.pallas_call(functools.partial(spread_kernel, row_count, col_count, buc...  67.5 us
    psum x1, blocking collectives, local(): total = lax.psum(jnp.sum(mine), ('px', 'py'))  49.7 us
    all_to_all x1, waiting for transfers between devices, local(): lax.all_to_all(mine, 'py', split_axis=1, concat_axis=0, tiled=True)  22.4 us
    all_gather x1, blocking collectives, local(): column = lax.all_gather(counts, 'px')  17.3 us
    dot_general x8, matrix products, dot(): return jnp.dot(a, b, preferred_element_type=jnp.float32)  11.1 us
    unnamed x34, local copies, waits for them, and re-layouts  8 us
  transfers between devices with their start and end apart: 3, of which 2 were waited for; matrix products, arithmetic and copies ran while one was open for 2% of the time, Pallas kernels for 0%

profile of v1, /device:TPU:0, one launch (start us, length us, event | category | flops | bytes accessed | tf_op | source)
XLA Modules:
  0.0 297.3 jit_solution(15886591064207621455)
XLA Ops:
  7.2 1.2 slice_reduce_fusion
  10.2 1.5 add_select_fusion
  11.9 67.5 %spread.1 = f32[8,272,1024]{2,1,0:T(8,128)S(1)} custom-call(s32[65]{0:T(128)S(1)} %convert_reduce_fusion.starts_ref, s32[648,128]{1,0:T(8,128)S(1)} %pad.23.lx_ref, s32[648,128]{1,0:T(8,128)S(1)} %pad.24.ly_ref, f32[648,128]{1,0:T(8,128)S(1)} %pad_convert_fusion.2.fx_ref, f32[648,128]{1,0:T(8,128)S(1)} %get-tuple-element.31.fy_ref, ...), custom_call_target="tpu_custom_call" | custom-call | tf_op jit(solution)/shard_map/spread/pallas_call | solution.py:98
  79.5 3.4 %copy-done = f32[8,272,1024]{2,1,0:T(8,128)} copy-done((f32[8,272,1024]{2,1,0:T(8,128)}, f32[8,272,1024]{2,1,0:T(8,128)S(1)}, u32[]{:S(2)}) %copy-start) | copy-done | bytes 8912920
  82.9 78.0 %reduce-scatter.2.cloned.1.call-done = f32[1,272,1024]{2,1,0:T(8,128)} async-done(((f32[8,272,1024]{2,1,0:T(8,128)}), f32[1,272,1024]{2,1,0:T(8,128)}) %reduce-scatter.2.cloned.1.call-update) | async-done | bytes 1114128 | tf_op jit(solution)/shard_map/reduce_scatter | solution.py:163
  160.9 1.8 all_to_all.15
  162.7 1.2 copy.24
  163.9 4.6 %all-to-all-start = ((f32[272,4,256]{2,0,1:T(8,128)}), f32[272,4,256]{2,0,1:T(8,128)S(1)}, u32[]{:S(2)}, u32[]{:S(2)}) async-start(f32[272,4,256]{2,0,1:T(8,128)} %copy.24), calls=%async_computation.1 | async-start | bytes 2228224 | tf_op jit(solution)/shard_map/all_to_all | solution.py:165
  168.6 4.5 %reduce-precision_convert_fusion.1 = (bf16[32,32,1024]{2,1,0:T(8,128)(2,1)}, bf16[32,32,1024]{2,1,0:T(8,128)(2,1)}, bf16[32,32,1024]{2,1,0:T(8,128)(2,1)}, bf16[32,32,1024]{2,1,0:T(8,128)(2,1)S(1)}) fusion(f32[32,1024]{1,0:T(8,128)S(1)} %copy-done.13, f32[32,1024]{1,0:T(8,128)} %constant.96.clone, f32[32,1024]{1,0:T(8,128)S(1)} %copy-done.14, ...), kind=kLoop, calls=%fused_computation.3 | loop fusion | flops 14680064 | bytes 8912896 | tf_op jit(solution)/shard_map/convert_element_type | solution.py:115
  173.1 22.4 %all-to-all-done = f32[272,4,256]{2,0,1:T(8,128)S(1)} async-done(((f32[272,4,256]{2,0,1:T(8,128)}), f32[272,4,256]{2,0,1:T(8,128)S(1)}, u32[]{:S(2)}, u32[]{:S(2)}) %all-to-all-start) | async-done | bytes 1114144 | tf_op jit(solution)/shard_map/all_to_all | solution.py:165
  195.8 1.3 copy-done.8
  197.1 1.2 fusion.10
  198.7 1.2 fusion.11
  201.7 1.5 maximum_bitcast_fusion
  203.2 2.9 all-to-all-start.1
  206.1 17.3 %all-gather = s32[8,1,64]{2,1,0:T(1,128)S(1)} all-gather(s32[1,1,64]{2,1,0:T(1,128)S(1)} %copy-done.15), channel_id=2, replica_groups=mesh['px'=8,'py'=4] {'px'}, dimensions={0}, use_global_device_ids=true | all-gather | bytes 2304 | tf_op jit(solution)/shard_map/all_gather | solution.py:206
  225.3 49.7 %psum.7 = f32[]{:T(128)} all-reduce(f32[]{:T(128)} %reduce_sum.41), channel_id=1, replica_groups=mesh['px'=8,'py'=4] {'px','py'}, use_global_device_ids=true, to_apply=%region_3.4 | all-reduce | flops 1 | bytes 8 | tf_op jit(solution)/shard_map/psum | solution.py:164
  275.7 1.4 copy.27
  278.0 1.1 copy-done.9
  279.2 2.3 fusion.7
  281.5 2.3 fusion.8
  285.5 1.3 fusion.3
  287.1 1.3 fusion.4
  288.9 1.6 fusion.5
  (63 shorter events, 9.9 us)
Async XLA Ops:
  7.2 4.6 %copy-start.10 = (s32[1,640,128]{2,1,0:T(8,128)S(1)}, s32[1,640,128]{2,1,0:T(8,128)}, u32[]{:S(2)}) copy-start(s32[1,640,128]{2,1,0:T(8,128)} %param.15) | copy-start | bytes 983044
  7.2 4.6 %copy-start.11 = (bf16[1,640,128]{2,1,0:T(8,128)(2,1)S(1)}, bf16[1,640,128]{2,1,0:T(8,128)(2,1)}, u32[]{:S(2)}) copy-start(bf16[1,640,128]{2,1,0:T(8,128)(2,1)} %param.14) | copy-start | bytes 491524
  7.2 4.7 %copy-start.12 = (bf16[1,640,128]{2,1,0:T(8,128)(2,1)S(1)}, bf16[1,640,128]{2,1,0:T(8,128)(2,1)}, u32[]{:S(2)}) copy-start(bf16[1,640,128]{2,1,0:T(8,128)(2,1)} %param.13) | copy-start | bytes 491524
  7.2 153.7 %reduce-scatter.2.cloned.1.call-start = ((), (), s32[]{:S(2)}) async-start(), calls=%async_computation.3 | async-start | bytes 10027008 | tf_op jit(solution)/shard_map/reduce_scatter | solution.py:163
  79.5 3.4 %copy-start = (f32[8,272,1024]{2,1,0:T(8,128)}, f32[8,272,1024]{2,1,0:T(8,128)S(1)}, u32[]{:S(2)}) copy-start(f32[8,272,1024]{2,1,0:T(8,128)S(1)} %spread.1) | copy-start | bytes 26738692
  162.7 5.9 %copy-start.13 = (f32[32,1024]{1,0:T(8,128)S(1)}, f32[32,1024]{1,0:T(8,128)}, u32[]{:S(2)}) copy-start(f32[32,1024]{1,0:T(8,128)} %constant.98.clone) | copy-start | bytes 393220
  162.7 5.9 %copy-start.14 = (f32[32,1024]{1,0:T(8,128)S(1)}, f32[32,1024]{1,0:T(8,128)}, u32[]{:S(2)}) copy-start(f32[32,1024]{1,0:T(8,128)} %constant.97.clone) | copy-start | bytes 393220
  163.9 31.6 %all-to-all-start = ((f32[272,4,256]{2,0,1:T(8,128)}), f32[272,4,256]{2,0,1:T(8,128)S(1)}, u32[]{:S(2)}, u32[]{:S(2)}) async-start(f32[272,4,256]{2,0,1:T(8,128)} %copy.24), calls=%async_computation.1 | async-start | bytes 2228224 | tf_op jit(solution)/shard_map/all_to_all | solution.py:165
  173.1 27.9 %copy-start.1 = (bf16[32,32,1024]{2,1,0:T(8,128)(2,1)}, bf16[32,32,1024]{2,1,0:T(8,128)(2,1)S(1)}, u32[]{:S(2)}) copy-start(bf16[32,32,1024]{2,1,0:T(8,128)(2,1)S(1)} %get-tuple-element.27) | copy-start | bytes 6291460
  195.5 1.6 copy-start.8
  197.1 1.6 copy-start.6
  198.7 1.6 copy-start.3
  203.2 2.9 copy-start.15
  203.2 20.7 %copy-start.5 = (f32[1,272,1024]{2,1,0:T(8,128)S(1)}, f32[1,272,1024]{2,1,0:T(8,128)}, u32[]{:S(2)}) copy-start(f32[1,272,1024]{2,1,0:T(8,128)} %reduce-scatter.2.cloned.1.call-done) | copy-start | bytes 3342340
  203.2 72.3 %all-to-all-start.1 = ((f32[32,2,32,256]{3,2,1,0:T(8,128)}), f32[32,2,32,256]{3,2,1,0:T(8,128)S(1)}, u32[]{:S(2)}, u32[]{:S(2)}) async-start(f32[32,2,32,256]{3,2,1,0:T(8,128)} %maximum_bitcast_fusion), calls=%async_computation.2 | async-start | bytes 4194304 | tf_op jit(solution)/shard_map/all_to_all | solution.py:185
  277.6 1.6 copy-start.9
  279.2 2.3 copy-start.7
  283.9 1.6 copy-start.4
  285.5 1.6 copy-start.2
Sparse Core Ops, SparseCore 0:
  83.0 77.7 reduce-scatter.1

commit v2 on v1

--- a/solution.py
+++ b/solution.py
@@ -134,6 +134,46 @@
     return jnp.dot(a, b, preferred_element_type=jnp.float32)
 
 
+def power_of(top):
+    return jnp.clip(jnp.floor(jnp.log2(jnp.maximum(top, 1e-30))) + 1.0, -90.0, 90.0).astype(jnp.int32)
+
+
+def scale_of(power):
+    return jnp.exp2((power - 15).astype(jnp.float32))
+
+
+def coded_as(value, power):
+    steps = jnp.round(value * jnp.exp2((15 - power).astype(jnp.float32)))
+    return jnp.clip(steps, -32767.0, 32767.0).astype(jnp.int16)
+
+
+def coded_rows(value, spare):
+    power = power_of(jnp.max(jnp.abs(value), axis=-2, keepdims=True))
+    row = lax.broadcasted_iota(jnp.int32, value.shape, value.ndim - 2)
+    return jnp.where(row == spare, power.astype(jnp.int16), coded_as(value, power))
+
+
+def plain_rows(coded, spare):
+    power = lax.slice_in_dim(coded, spare, spare + 1, axis=coded.ndim - 2).astype(jnp.int32)
+    row = lax.broadcasted_iota(jnp.int32, coded.shape, coded.ndim - 2)
+    return jnp.where(row == spare, 0.0, coded.astype(jnp.float32) * scale_of(power))
+
+
+def digits(value, width):
+    power = power_of(value)
+    scaled = value * jnp.exp2((14 - power).astype(jnp.float32))
+    high = jnp.clip(jnp.floor(scaled), 0.0, 32767.0)
+    low = jnp.clip(jnp.floor((scaled - high) * 16384.0), 0.0, 16384.0)
+    lane = lax.broadcasted_iota(jnp.int32, (1, width), 1)
+    rest = jnp.where(lane == 1, high, low).astype(jnp.int32)
+    return jnp.where(lane == 0, power, rest)
+
+
+def number(row):
+    value = row[..., 1].astype(jnp.float32) + row[..., 2].astype(jnp.float32) / 16384.0
+    return value * jnp.exp2((row[..., 0] - 14).astype(jnp.float32))
+
+
 def local(cell_ids, offset_x, offset_y, mass, live, tile_owner, counts):
     px_count = lax.axis_size("px")
     py_count = lax.axis_size("py")
@@ -159,12 +199,23 @@
     width = NX // parts
     if parts > 1:
         grid = grid.reshape(PLANES, height, parts, width).transpose(0, 2, 1, 3)
-        grid = grid.reshape(px_count, height, width)
-    mine = lax.psum_scatter(grid, "px", scatter_dimension=0, tiled=True)[0]
-    total = lax.psum(jnp.sum(mine), ("px", "py"))
-    by_cols = lax.all_to_all(mine, "py", split_axis=1, concat_axis=0, tiled=True)
+    grid = grid.reshape(px_count // 2, 2, height, width)
+    side = lax.axis_index("px") % 2
+    keep = lax.dynamic_index_in_dim(grid, side, 1, keepdims=False)
+    away = lax.dynamic_index_in_dim(grid, 1 - side, 1, keepdims=False)
+    pairs = [(source, source ^ 1) for source in range(px_count)]
+    summed = keep + lax.ppermute(away, "px", pairs)
+    groups = [list(range(k, px_count, 2)) for k in range(2)]
+    got = lax.all_to_all(
+        coded_rows(summed, col_count + 8), "px", 0, 0, axis_index_groups=groups, tiled=True
+    )
+    mine = jnp.sum(plain_rows(got, col_count + 8), axis=0)
+    total = jnp.sum(mine)
+    by_cols = lax.all_to_all(
+        coded_rows(mine, col_count + 8), "py", split_axis=1, concat_axis=0, tiled=True
+    )
     part = width // py_count
-    ext = by_cols.reshape(py_count, height, part)
+    ext = plain_rows(by_cols.reshape(py_count, height, part), col_count + 8)
     core = ext[:, :col_count]
     right = jnp.roll(ext[:, col_count : col_count + 4], 1, axis=0)
     left = jnp.roll(ext[:, col_count + 12 :], -1, axis=0)
@@ -181,9 +232,30 @@
     imag = -(imag[:, :part] + imag[:, part:] + dot(sin_lo, hi))
     devices = px_count * py_count
     ky_part = NY // devices
-    lines = jnp.stack([real, imag]).reshape(2, devices, ky_part, part).transpose(1, 0, 2, 3)
-    got = lax.all_to_all(lines, ("px", "py"), split_axis=0, concat_axis=0, tiled=True)
-    got = got.reshape(PLANES, parts * py_count, 2, ky_part, part).transpose(2, 0, 3, 1, 4)
+    lines = jnp.stack([real.reshape(devices, ky_part, part), imag.reshape(devices, ky_part, part)], 1)
+    lines = lines.reshape(devices, 2 * ky_part, part)
+    power = power_of(jnp.max(jnp.abs(lines), axis=1, keepdims=True))
+    coded = coded_as(lines, power)
+    bucket_count = counts.shape[-1]
+    count_rows = -(-bucket_count // part)
+    spare = -(2 + count_rows) % 8
+    side_rows = jnp.concatenate(
+        [
+            digits(total, part),
+            jnp.pad(counts.reshape(-1), (0, count_rows * part - bucket_count)).reshape(-1, part),
+            jnp.zeros((spare, part), jnp.int32),
+        ]
+    ).astype(jnp.int16)
+    side_rows = jnp.broadcast_to(side_rows[None], (devices,) + side_rows.shape)
+    coded = jnp.concatenate([coded, power.astype(jnp.int16), side_rows], axis=1)
+    got = lax.all_to_all(coded, ("px", "py"), split_axis=0, concat_axis=0, tiled=True)
+    after = got[:, 2 * ky_part :].astype(jnp.int32)
+    lines = got[:, : 2 * ky_part].astype(jnp.float32) * scale_of(after[:, :1])
+    total = jnp.sum(number(after[:, 1]))
+    column = after[:, 2 : 2 + count_rows].reshape(px_count, py_count, 1, count_rows * part)
+    column = lax.dynamic_index_in_dim(column, lax.axis_index("py"), 1, keepdims=False)
+    column = column[:, :, :bucket_count][:, None]
+    got = lines.reshape(PLANES, parts * py_count, 2, ky_part, part).transpose(2, 0, 3, 1, 4)
     got = got.reshape(2 * PLANES * ky_part, NX)
     hi, lo = split(got)
     rows = PLANES * ky_part
@@ -203,7 +275,6 @@
         & (lax.broadcasted_iota(jnp.int32, shape, 3) == 0)
     )
     spectrum = out * (PLANES * NX * NY * norm / total) - jnp.where(at_zero, NX * NY * norm, 0.0)
-    column = lax.all_gather(counts, "px")
     column_sum = jnp.sum(column, axis=0)
     reached = lax.broadcasted_iota(jnp.int32, column.shape, 0) < lax.axis_index("px")
     earlier = jnp.sum(jnp.where(reached, column, 0), axis=0)

time: 298 us -> 218 us (0.73)
  waiting for transfers between devices: 100 us -> 43.5 us
  blocking collectives: 67 us -> 33.4 us
  other arithmetic: 14.3 us -> 26.4 us
  between operations: 15 us -> 3.3 us
  matrix products: 11.1 us -> 17.5 us
    reduce_scatter x1 -> x0, waiting for transfers between devices: 78 us -> none  [local(): mine = lax.psum_scatter(grid, 'px', scatter_dimension=0, tiled=True)[0]]
    psum x1 -> x0, blocking collectives: 49.7 us -> none  [local(): total = lax.psum(jnp.sum(mine), ('px', 'py'))]
    all_to_all x0 -> x1, blocking collectives: none -> 33.4 us  [local(): lax.all_to_all(coded_rows(summed, col_count + 8), 'px', 0, 0, axis_index_...]
    all_gather x1 -> x0, blocking collectives: 17.3 us -> none  [local(): column = lax.all_gather(counts, 'px')]
    all_to_all x2, waiting for transfers between devices: 22.4 us -> 35.6 us  [the longest x1 27.3 us: local(): lax.all_to_all(coded, ('px', 'py'), split_axis=0, concat_axis=0, tiled=True)]
    ppermute x0 -> x1, waiting for transfers between devices: none -> 7.87 us  [local(): summed = keep + lax.ppermute(away, 'px', pairs)]
    dot_general x8, matrix products: 11.1 us -> 17.5 us  [dot(): return jnp.dot(a, b, preferred_element_type=jnp.float32)]
    reduce_max x0 -> x2, other arithmetic: none -> 4.91 us  [coded_rows(): power = power_of(jnp.max(jnp.abs(value), axis=-2, keepdims=True))]
  transfers between devices with their start and end apart: 3 -> 3, of which waited for: 2 -> 3; matrix products, arithmetic and copies ran while one was open for 2% -> 2% of each run, Pallas kernels for 0% -> 0%
where the time goes in v2:
time: 218 us; the launch traced here: 216 us
  Pallas kernels  69 us (32%)
  waiting for transfers between devices  43.5 us (20%)
  blocking collectives  33.4 us (15%)
  other arithmetic  26.4 us (12%)
  matrix products  17.5 us (8%)
  local copies, waits for them, and re-layouts  16.2 us (7%)
  starting transfers between devices  6.61 us (3%)
  between operations  3.3 us (2%)
    pallas_call x1, Pallas kernels, spread(): pl.pallas_call(functools.partial(spread_kernel, row_count, col_count, buc...  69 us
    all_to_all x1, blocking collectives, local(): lax.all_to_all(coded_rows(summed, col_count + 8), 'px', 0, 0, axis_index_...  33.4 us
    all_to_all x1, waiting for transfers between devices, local(): lax.all_to_all(coded, ('px', 'py'), split_axis=0, concat_axis=0, tiled=True)  27.3 us
    dot_general x8, matrix products, dot(): return jnp.dot(a, b, preferred_element_type=jnp.float32)  17.5 us
    all_to_all x1, waiting for transfers between devices, local(): lax.all_to_all(coded_rows(mine, col_count + 8), 'py', split_axis=1, conca...  8.36 us
    unnamed x44, local copies, waits for them, and re-layouts  8.06 us
    ppermute x1, waiting for transfers between devices, local(): summed = keep + lax.ppermute(away, 'px', pairs)  7.87 us
    convert_element_type x5, other arithmetic, split(): return (high.astype(jnp.bfloat16), (value - high).astype(jnp.bfloat16))  6 us
  transfers between devices with their start and end apart: 3, of which 3 were waited for; matrix products, arithmetic and copies ran while one was open for 2% of the time, Pallas kernels for 0%

profile of v2, /device:TPU:0, one launch (start us, length us, event | category | flops | bytes accessed | tf_op | source)
XLA Modules:
  0.0 215.7 jit_solution(2302986730504060030)
XLA Ops:
  2.6 1.5 add_select_fusion
  4.5 69.0 %spread.1 = f32[8,272,1024]{2,1,0:T(8,128)S(1)} custom-call(s32[65]{0:T(128)S(1)} %convert_reduce_fusion.starts_ref, s32[648,128]{1,0:T(8,128)S(1)} %pad.28.lx_ref, s32[648,128]{1,0:T(8,128)S(1)} %pad.29.ly_ref, f32[648,128]{1,0:T(8,128)S(1)} %pad_convert_fusion.2.fx_ref, f32[648,128]{1,0:T(8,128)S(1)} %get-tuple-element.45.fy_ref, ...), custom_call_target="tpu_custom_call" | custom-call | tf_op jit(solution)/shard_map/spread/pallas_call | solution.py:98
  73.5 3.1 %dynamic-slice_bitcast_fusion = f32[4,272,1024]{2,1,0:T(8,128)} fusion(f32[4,2,272,1024]{3,2,1,0:T(8,128)S(1)} %bitcast.88, s32[]{:T(128)S(6)} %select_n.128), kind=kLoop, calls=%fused_computation.10 | loop fusion | bytes 8912900 | tf_op jit(solution)/shard_map/jit(dynamic_index_in_dim)/squeeze | solution.py:205
  76.6 1.6 copy-done
  78.2 7.9 %collective-permute-done = f32[4,272,1024]{2,1,0:T(8,128)} collective-permute-done((f32[4,272,1024]{2,1,0:T(8,128)}, f32[4,272,1024]{2,1,0:T(8,128)}, u32[]{:S(2)}, u32[]{:S(2)}) %collective-permute-start) | collective-permute-done | bytes 4456480 | tf_op jit(solution)/shard_map/ppermute | solution.py:207
  86.1 4.8 %abs_reduce_fusion = f32[4,1024]{1,0:T(4,128)S(1)} fusion(f32[4,272,1024]{2,1,0:T(8,128)} %collective-permute-done, f32[4,2,272,1024]{3,2,1,0:T(8,128)} %bitcast.89, s32[]{:T(128)S(6)} %select_n.127), kind=kLoop, calls=%fused_computation.9 | loop fusion | flops 3338240 | bytes 8929284 | tf_op jit(solution)/shard_map/reduce_max | solution.py:151
  91.0 1.3 copy-done.1
  92.2 3.5 %fusion.4 = s16[4,272,1024]{2,1,0:T(8,128)(2,1)S(1)} fusion(f32[4,1024]{1,0:T(4,128)S(1)} %get-tuple-element.39, pred[272]{0:T(512)(128)(4,1)S(1)} %iota_compare_fusion.2, f32[4,272,1024]{2,1,0:T(8,128)} %collective-permute-done, f32[4,2,272,1024]{3,2,1,0:T(8,128)S(1)} %bitcast.90, s32[]{:T(128)S(6)} %select_n.127, s16[4,1024]{1,0:T(4,128)(2,1)S(1)} %get-tuple-element.38), kind=kLoop, calls=%fused_computation.17 | loop fusion | flops 6684672 | bytes 11165972 | tf_op jit(solution)/shard_map/jit(_where)/select_n | solution.py:153
  95.8 33.4 %all_to_all.23 = s16[4,272,1024]{2,1,0:T(8,128)(2,1)S(1)} all-to-all(s16[4,272,1024]{2,1,0:T(8,128)(2,1)S(1)} %fusion.4), channel_id=1, replica_groups={{0,8,16,24},{4,12,20,28},{1,9,17,25},{5,13,21,29},{2,10,18,26},{6,14,22..., dimensions={0} | all-to-all | bytes 4456448 | tf_op jit(solution)/shard_map/all_to_all | solution.py:209
  129.2 2.1 fusion.1
  134.0 3.7 %all-to-all-start.1 = ((s16[272,4,256]{2,0,1:T(8,128)(2,1)}), s16[272,4,256]{2,0,1:T(8,128)(2,1)S(1)}, u32[]{:S(2)}, u32[]{:S(2)}) async-start(s16[272,4,256]{2,0,1:T(8,128)(2,1)} %copy.38), calls=%async_computation.1 | async-start | bytes 1114112 | tf_op jit(solution)/shard_map/all_to_all | solution.py:214
  137.9 3.8 %reduce-precision_convert_fusion.1 = (bf16[32,32,1024]{2,1,0:T(8,128)(2,1)}, bf16[32,32,1024]{2,1,0:T(8,128)(2,1)}, bf16[32,32,1024]{2,1,0:T(8,128)(2,1)S(1)}, bf16[32,32,1024]{2,1,0:T(8,128)(2,1)}) fusion(f32[32,1024]{1,0:T(8,128)S(1)} %copy-done.16, f32[32,1024]{1,0:T(8,128)S(1)} %copy-done.14, f32[32,1024]{1,0:T(8,128)S(1)} %copy-done.15, ...), kind=kLoop, calls=%fused_computation.3 | loop fusion | flops 14680064 | bytes 8912896 | tf_op jit(solution)/shard_map/convert_element_type | solution.py:115
  143.2 8.4 %all-to-all-done.1 = s16[272,4,256]{2,0,1:T(8,128)(2,1)S(1)} async-done(((s16[272,4,256]{2,0,1:T(8,128)(2,1)}), s16[272,4,256]{2,0,1:T(8,128)(2,1)S(1)}, u32[]{:S(2)}, u32[]{:S(2)}) %all-to-all-start.1) | async-done | bytes 557088 | tf_op jit(solution)/shard_map/all_to_all | solution.py:214
  153.4 1.2 fusion.18
  159.9 2.9 %all-to-all-start.2 = ((s16[32,72,256]{2,1,0:T(8,128)(2,1)}), s16[32,72,256]{2,1,0:T(8,128)(2,1)S(1)}, u32[]{:S(2)}, u32[]{:S(2)}) async-start(s16[32,72,256]{2,1,0:T(8,128)(2,1)} %pad_add_fusion), calls=%async_computation.2 | async-start | bytes 2359296 | tf_op jit(solution)/shard_map/all_to_all | solution.py:251
  163.0 27.3 %all-to-all-done.2 = s16[32,72,256]{2,1,0:T(8,128)(2,1)S(1)} async-done(((s16[32,72,256]{2,1,0:T(8,128)(2,1)}), s16[32,72,256]{2,1,0:T(8,128)(2,1)S(1)}, u32[]{:S(2)}, u32[]{:S(2)}) %all-to-all-start.2) | async-done | bytes 1179680 | tf_op jit(solution)/shard_map/all_to_all | solution.py:251
  191.4 1.4 copy.43
  192.8 1.4 fusion.9
  196.3 4.3 %fusion.15 = f32[1024,1024]{1,0:T(8,128)} fusion(bf16[1024,1024]{1,0:T(8,128)(2,1)S(1)} %bitcast.110, bf16[512,1024]{1,0:T(8,128)(2,1)S(1)} %get-tuple-element.19, bf16[512,1024]{1,0:T(8,128)(2,1)S(1)} %get-tuple-element.18), kind=kOutput, calls=%fused_computation.41 | convolution fusion | flops 2151677952 | bytes 8388608 | tf_op jit(solution)/shard_map/dot_general | solution.py:134
  200.6 4.3 %fusion.14 = f32[1024,1024]{1,0:T(8,128)} fusion(bf16[1024,1024]{1,0:T(8,128)(2,1)S(1)} %bitcast.108, bf16[512,1024]{1,0:T(8,128)(2,1)S(1)} %get-tuple-element.19, bf16[512,1024]{1,0:T(8,128)(2,1)S(1)} %get-tuple-element.18), kind=kOutput, calls=%fused_computation.40 | convolution fusion | flops 2151677952 | bytes 8388608 | tf_op jit(solution)/shard_map/dot_general | solution.py:134
  205.4 1.4 copy-done.3
  206.8 3.7 %fusion.7 = f32[512,1024]{1,0:T(8,128)S(1)} fusion(f32[1024,1024]{1,0:T(8,128)} %fusion.15, bf16[512,1024]{1,0:T(8,128)(2,1)S(1)} %bitcast.112, bf16[1024,1024]{1,0:T(8,128)(2,1)S(1)} %bitcast.96), kind=kOutput, calls=%fused_computation.22 | convolution fusion | flops 1074790400 | bytes 9437184 | tf_op jit(solution)/shard_map/dot_general | solution.py:134
  210.5 1.3 fusion.6
  214.2 1.6 fusion.8
  (103 shorter events, 17.6 us)
Async XLA Ops:
  0.6 3.7 %copy-start.11 = (bf16[1,640,128]{2,1,0:T(8,128)(2,1)S(1)}, bf16[1,640,128]{2,1,0:T(8,128)(2,1)}, u32[]{:S(2)}) copy-start(bf16[1,640,128]{2,1,0:T(8,128)(2,1)} %param.12) | copy-start | bytes 491524
  0.6 3.7 %copy-start.10 = (bf16[1,640,128]{2,1,0:T(8,128)(2,1)S(1)}, bf16[1,640,128]{2,1,0:T(8,128)(2,1)}, u32[]{:S(2)}) copy-start(bf16[1,640,128]{2,1,0:T(8,128)(2,1)} %param.14) | copy-start | bytes 491524
  0.7 3.7 %copy-start.8 = (s32[1,640,128]{2,1,0:T(8,128)S(1)}, s32[1,640,128]{2,1,0:T(8,128)}, u32[]{:S(2)}) copy-start(s32[1,640,128]{2,1,0:T(8,128)} %param.15) | copy-start | bytes 983044
  0.7 3.8 %copy-start.12 = (bf16[1,640,128]{2,1,0:T(8,128)(2,1)S(1)}, bf16[1,640,128]{2,1,0:T(8,128)(2,1)}, u32[]{:S(2)}) copy-start(bf16[1,640,128]{2,1,0:T(8,128)(2,1)} %param.13) | copy-start | bytes 491524
  73.5 4.8 %copy-start = (f32[8,272,1024]{2,1,0:T(8,128)}, f32[8,272,1024]{2,1,0:T(8,128)S(1)}, u32[]{:S(2)}) copy-start(f32[8,272,1024]{2,1,0:T(8,128)S(1)} %spread.1) | copy-start | bytes 26738692
  78.2 7.9 %collective-permute-start = (f32[4,272,1024]{2,1,0:T(8,128)}, f32[4,272,1024]{2,1,0:T(8,128)}, u32[]{:S(2)}, u32[]{:S(2)}) collective-permute-start(f32[4,272,1024]{2,1,0:T(8,128)} %dynamic-slice_bitcast_fusion), channel_id=1, source_target_pairs={{0,4},{4,0},{8,12},{12,8},{16,20},{20,16},{24,28},{28,24},{1,5},{5... | collective-permute-start | bytes 13369352 | tf_op jit(solution)/shard_map/ppermute | solution.py:207
  86.1 6.1 %copy-start.1 = (f32[8,272,1024]{2,1,0:T(8,128)S(1)}, f32[8,272,1024]{2,1,0:T(8,128)}, u32[]{:S(2)}) copy-start(f32[8,272,1024]{2,1,0:T(8,128)} %copy-done) | copy-start | bytes 26738692
  132.0 5.7 %copy-start.18 = (s32[1,1,64]{2,1,0:T(1,128)S(1)}, s32[1,1,64]{2,1,0:T(1,128)}, u32[]{:S(2)}) copy-start(s32[1,1,64]{2,1,0:T(1,128)} %param.17) | copy-start | bytes 772
  132.0 5.9 %copy-start.13 = (f32[32,1024]{1,0:T(8,128)S(1)}, f32[32,1024]{1,0:T(8,128)}, u32[]{:S(2)}) copy-start(f32[32,1024]{1,0:T(8,128)} %constant.178.clone) | copy-start | bytes 393220
  132.0 5.8 %copy-start.14 = (f32[32,1024]{1,0:T(8,128)S(1)}, f32[32,1024]{1,0:T(8,128)}, u32[]{:S(2)}) copy-start(f32[32,1024]{1,0:T(8,128)} %constant.179.clone) | copy-start | bytes 393220
  132.0 5.8 %copy-start.15 = (f32[32,1024]{1,0:T(8,128)S(1)}, f32[32,1024]{1,0:T(8,128)}, u32[]{:S(2)}) copy-start(f32[32,1024]{1,0:T(8,128)} %constant.180.clone) | copy-start | bytes 393220
  132.0 5.8 %copy-start.16 = (f32[32,1024]{1,0:T(8,128)S(1)}, f32[32,1024]{1,0:T(8,128)}, u32[]{:S(2)}) copy-start(f32[32,1024]{1,0:T(8,128)} %constant.181.clone) | copy-start | bytes 393220
  134.0 17.5 %all-to-all-start.1 = ((s16[272,4,256]{2,0,1:T(8,128)(2,1)}), s16[272,4,256]{2,0,1:T(8,128)(2,1)S(1)}, u32[]{:S(2)}, u32[]{:S(2)}) async-start(s16[272,4,256]{2,0,1:T(8,128)(2,1)} %copy.38), calls=%async_computation.1 | async-start | bytes 1114112 | tf_op jit(solution)/shard_map/all_to_all | solution.py:214
  151.8 1.6 copy-start.6
  153.4 1.6 copy-start.4
  155.0 1.6 copy-start.2
  159.9 30.4 %all-to-all-start.2 = ((s16[32,72,256]{2,1,0:T(8,128)(2,1)}), s16[32,72,256]{2,1,0:T(8,128)(2,1)S(1)}, u32[]{:S(2)}, u32[]{:S(2)}) async-start(s16[32,72,256]{2,1,0:T(8,128)(2,1)} %pad_add_fusion), calls=%async_computation.2 | async-start | bytes 2359296 | tf_op jit(solution)/shard_map/all_to_all | solution.py:251
  194.7 1.6 copy-start.7
  196.3 4.3 %copy-start.5 = (bf16[32,32,1024]{2,1,0:T(8,128)(2,1)S(1)}, bf16[32,32,1024]{2,1,0:T(8,128)(2,1)}, u32[]{:S(2)}) copy-start(bf16[32,32,1024]{2,1,0:T(8,128)(2,1)} %get-tuple-element.29) | copy-start | bytes 6291460
  200.6 4.3 %copy-start.17 = (s32[32,1,256]{2,0,1:T(8,128)S(1)}, s32[32,1,256]{2,0,1:T(8,128)}, u32[]{:S(2)}) copy-start(s32[32,1,256]{2,0,1:T(8,128)} %get-tuple-element.34) | copy-start | bytes 98308
  205.2 1.6 copy-start.3
  206.8 3.7 %copy-start.19 = (f32[1024,1024]{1,0:T(8,128)S(1)}, f32[1024,1024]{1,0:T(8,128)}, u32[]{:S(2)}) copy-start(f32[1024,1024]{1,0:T(8,128)} %fusion.14) | copy-start | bytes 12582916
  210.5 1.3 copy-start.9
